TPU v7x, 32 devices: a whole 2x2x4 slice. The times are simulated.
32 devices in a mesh: seq: 16 (over z, y, x), head: 2 (over core).
Axes of the slice: x: 2, y: 2, z: 4, core: 2. Of those that a mesh axis runs over, the one named last changes fastest.
Arguments:
- hidden_state: bfloat16 [8, 4096], replicated, may hold values from -18 to 18
- query_weight: bfloat16 [4096, 2, 2048], P('seq', 'head'), may hold values from -1 to 1
- up_key: bfloat16 [2, 256, 512], P('head'), may hold values from -1 to 1
- up_value: bfloat16 [2, 256, 512], P('head'), may hold values from -0.375 to 0.375
- latent_key: bfloat16 [8, 16384, 2, 256], P(None, 'seq', 'head'), may hold values from -256 to 256
- latent_value: bfloat16 [8, 16384, 2, 256], P(None, 'seq', 'head'), may hold values from -6 to 6
- lengths: int32 [8], replicated, may hold values from 12288 to 16384
- block_mask: int32 [8, 64], P(None, 'seq'), may hold values from 0 to 1, as said below
- out_weight: bfloat16 [2, 2048, 4096], P('head', 'seq'), may hold values from -0.09375 to 0.09375
Outputs:
- attn_out: float32 [8, 4096], replicated
Inputs may be any that keep to these rules, and one draw needn't show every extreme that they name: `block_mask`: blocks 0 and 32 of every sequence are valid.
All inputs are finite; a program needn't handle non-finite values.
Results may differ from a plain program's by a relative error of at most 0.0035.
Values sent between devices are 32-bit elements; how exact they have to be, the bound alone decides.
No kernel may reach another device: no remote copies, remote signals or barrier semaphores. Data moves between devices by JAX's collectives and lax.ppermute only.
A program may use at most 64 MiB of HBM per device.

v0:
```python
import math
import jax
import jax.numpy as jnp
from jax import lax
from jax.sharding import PartitionSpec as P

HD = 128
R = 256
BLOCK = 256
KPG = 4
REP = 4
QW = 2048


def joined(part, axis, combine):
    gathered = jax.tree.map(lambda a: lax.all_gather(a, axis), part)

    def take(source):
        return jax.tree.map(lambda a: lax.dynamic_index_in_dim(a, source, 0, False), gathered)

    return lax.fori_loop(
        1, lax.axis_size(axis), lambda source, state: combine(state, take(source)), take(0)
    )


def join_carries(earlier, later):
    peak_a, total_a, summed_a = earlier
    peak_b, total_b, summed_b = later
    peak = jnp.maximum(peak_a, peak_b)
    factor_a = jnp.exp(peak_a - peak)
    factor_b = jnp.exp(peak_b - peak)
    total = total_a * factor_a + total_b * factor_b
    summed = summed_a * factor_a[..., None] + summed_b * factor_b[..., None]
    return (peak, total, summed)


def body(
    hidden_state,
    query_weight,
    up_key,
    up_value,
    latent_key,
    latent_value,
    lengths,
    block_mask,
    out_weight,
):
    highest = lax.Precision.HIGHEST
    seq_index = lax.axis_index("seq")
    batch = hidden_state.shape[0]
    dim_rows = query_weight.shape[0]
    state_rows = lax.dynamic_slice_in_dim(hidden_state, seq_index * dim_rows, dim_rows, 1)
    partial_query = jnp.dot(state_rows, query_weight[:, 0, :], preferred_element_type=jnp.float32)
    query = lax.psum(partial_query, "seq")
    query_heads = query.reshape(batch, KPG, REP, HD)
    keys_lat = latent_key[:, :, 0, :]
    values_lat = latent_value[:, :, 0, :]
    context_len = keys_lat.shape[1]
    positions = seq_index * context_len + jnp.arange(context_len, dtype=jnp.int32)
    block_full = jnp.repeat(block_mask, BLOCK, axis=1)
    valid = (positions[None, :] < lengths[:, None]) & (block_full > 0)
    mask_heads = valid[:, None, None, :]
    scale = 1.0 / math.sqrt(HD)
    key_maps = up_key[0].astype(jnp.float32).reshape(R, KPG, HD)
    query_latent = jnp.einsum("bjrd,ejd->bjre", query_heads, key_maps, precision=highest)
    scores = (
        jnp.einsum("bjre,bce->bjrc", query_latent, keys_lat.astype(jnp.float32), precision=highest)
        * scale
    )
    peak = jnp.max(jnp.where(mask_heads, scores, -1e30), axis=-1)
    weights = jnp.where(mask_heads, jnp.exp(scores - peak[..., None]), 0.0)
    total = jnp.sum(weights, axis=-1)
    value_maps = up_value[0].astype(jnp.float32).reshape(R, KPG, HD)
    latent_sum = jnp.einsum(
        "bjrc,bce->bjre", weights, values_lat.astype(jnp.float32), precision=highest
    )
    summed = jnp.einsum("bjre,ejd->bjrd", latent_sum, value_maps, precision=highest)
    out_rows = out_weight.shape[1]
    peak_all, total_all, summed_all = joined((peak, total, summed), "seq", join_carries)
    context = (summed_all / total_all[..., None]).reshape(batch, QW).astype(jnp.bfloat16)
    context_rows = lax.dynamic_slice_in_dim(context, seq_index * out_rows, out_rows, 1)
    partial_out = jnp.dot(context_rows, out_weight[0], preferred_element_type=jnp.float32)
    return lax.psum(partial_out, ("seq", "head"))


def solution(mesh):
    in_specs = (
        P(),
        P("seq", "head", None),
        P("head", None, None),
        P("head", None, None),
        P(None, "seq", "head", None),
        P(None, "seq", "head", None),
        P(),
        P(None, "seq"),
        P("head", "seq", None),
    )
    out_specs = P()
    return jax.shard_map(body, mesh=mesh, in_specs=in_specs, out_specs=out_specs, check_vma=False)
```

profile of v0, /device:TPU:0, one launch (start us, length us, event | category | flops | bytes accessed | tf_op | source)
XLA Modules:
  0.0 361.0 jit_solution(18013315302296954894)
XLA Ops:
  6.5 1.6 fusion.13
  8.1 0.7 copy.28
  8.8 0.7 broadcast_compare_fusion
  9.6 0.7 compare_and_fusion
  10.3 1.0 reshape.54
  11.4 1.0 reshape.55
  12.4 106.7 %all-reduce.3.cloned.1.call-done = f32[8,4,4,128]{3,2,1,0:T(4,128)} async-done(((f32[8,4,4,128]{3,2,1,0:T(4,128)}), f32[8,4,4,128]{3,2,1,0:T(4,128)}) %all-reduce.3.cloned.1.call-update) | async-done | bytes 65552 | tf_op jit(solution)/shard_map/psum | solution.py:54
  119.1 1.4 convolution_bitcast_fusion
  120.4 5.7 %select_reduce_fusion = (f32[8,4,4]{2,1,0:T(4,128)S(1)}, f32[8,4,4,1024]{3,2,1,0:T(4,128)S(1)}) fusion(pred[8,1024]{1,0:T(8,128)(4,1)S(1)} %compare_and_fusion, f32[8,4,4,256]{3,2,1,0:T(4,128)S(1)} %convolution_bitcast_fusion, bf16[8,1024,1,256]{3,1,2,0:T(8,128)(2,1)} %param.15), kind=kOutput, calls=%fused_computation.22 | convolution fusion | flops 403046272 | bytes 4858368 | tf_op jit(solution)/shard_map/bjre,bce->bjrc/dot_general | solution.py:67
  126.1 2.1 fusion.4
  128.2 0.9 convolution_bitcast_fusion.1
  129.2 40.4 %all-gather = f32[128,4,4]{2,1,0:T(4,128)S(1)} all-gather(f32[8,4,4]{2,1,0:T(4,128)S(1)} %get-tuple-element.223), channel_id=2, replica_groups=mesh['seq'=16,'head'=2] {'seq'}, dimensions={0}, use_global_device_ids=true | all-gather | bytes 8704 | tf_op jit(solution)/shard_map/all_gather | solution.py:16
  169.8 0.5 copy.37
  170.2 0.4 fusion.15
  170.6 37.1 %all-gather.1 = f32[128,4,4]{2,1,0:T(4,128)S(1)} all-gather(f32[8,4,4]{2,1,0:T(4,128)S(1)} %fusion.15), channel_id=3, replica_groups=mesh['seq'=16,'head'=2] {'seq'}, dimensions={0}, use_global_device_ids=true | all-gather | bytes 8704 | tf_op jit(solution)/shard_map/all_gather | solution.py:16
  207.9 0.5 copy.38
  208.4 0.8 slice.8
  209.2 20.1 %while.19 = (s32[]{:T(128)}, f32[8,4,4]{0,2,1:T(4,128)S(1)}, f32[8,4,4]{0,2,1:T(4,128)S(1)}, f32[8,4,4,128]{3,2,1,0:T(4,128)S(1)}, f32[16,8,4,4]{1,3,2,0:T(4,128...) while((s32[]{:T(128)}, f32[8,4,4]{0,2,1:T(4,128)S(1)}, ...), condition=%wide.region_4.5_spmd, body=%wide.region_3.4_spmd.sunk | while | flops 49925 | bytes 334991 | solution.py:21
  209.5 0.8 constant_dynamic-slice_fusion.2
  210.3 0.2 fusion.34
  210.8 0.8 constant_dynamic-slice_fusion.2
  211.7 0.2 fusion.34
  212.2 0.8 constant_dynamic-slice_fusion.2
  213.0 0.2 fusion.34
  213.5 0.8 constant_dynamic-slice_fusion.2
  214.4 0.2 fusion.34
  214.9 0.8 constant_dynamic-slice_fusion.2
  215.7 0.2 fusion.34
  216.2 0.8 constant_dynamic-slice_fusion.2
  217.0 0.2 fusion.34
  217.5 0.8 constant_dynamic-slice_fusion.2
  218.4 0.2 fusion.34
  218.9 0.8 constant_dynamic-slice_fusion.2
  219.7 0.2 fusion.34
  220.2 0.8 constant_dynamic-slice_fusion.2
  221.1 0.2 fusion.34
  221.5 0.8 constant_dynamic-slice_fusion.2
  222.9 0.8 constant_dynamic-slice_fusion.2
  224.2 0.8 constant_dynamic-slice_fusion.2
  225.1 0.2 fusion.34
  225.6 0.8 constant_dynamic-slice_fusion.2
  226.4 0.2 fusion.34
  226.9 0.8 constant_dynamic-slice_fusion.2
  228.2 0.8 constant_dynamic-slice_fusion.2
  229.1 0.2 fusion.34
  229.6 0.9 fusion.11
  230.5 122.4 %all-reduce.5.cloned.1.call-done = f32[8,4096]{1,0:T(8,128)} async-done(((f32[8,4096]{1,0:T(8,128)}), f32[8,4096]{1,0:T(8,128)}) %all-reduce.5.cloned.1.call-update) | async-done | bytes 131088 | tf_op jit(solution)/shard_map/psum | solution.py:83
  352.9 1.6 copy.84
  (69 shorter events, 5.0 us)
Async XLA Ops:
  6.5 223.1 %copy-start = (bf16[1,128,4096]{2,1,0:T(8,128)(2,1)S(1)}, bf16[1,128,4096]{2,1,0:T(8,128)(2,1)}, u32[]{:S(2)}) copy-start(bf16[1,128,4096]{2,1,0:T(8,128)(2,1)} %param.19) | copy-start | bytes 3145732
  6.5 112.5 %all-reduce.3.cloned.1.call-start = ((), (), s32[]{:S(2)}) async-start(), calls=%async_computation | async-start | bytes 131072 | tf_op jit(solution)/shard_map/psum | solution.py:54
  8.8 199.6 %all-gather.5.cloned.1.call-start = ((), (), s32[]{:S(2)}) async-start(), calls=%async_computation.2 | async-start | bytes 1114112 | tf_op jit(solution)/shard_map/all_gather | solution.py:16
  119.1 7.0 %copy-start.1 = (bf16[8,1024,1,256]{3,1,2,0:T(8,128)(2,1)S(1)}, bf16[8,1024,1,256]{3,1,2,0:T(8,128)(2,1)}, u32[]{:S(2)}) copy-start(bf16[8,1024,1,256]{3,1,2,0:T(8,128)(2,1)} %param.16) | copy-start | bytes 12582916
  129.2 223.8 %all-reduce.5.cloned.1.call-start = ((), (), s32[]{:S(2)}) async-start(), calls=%async_computation.1 | async-start | bytes 262144 | tf_op jit(solution)/shard_map/psum | solution.py:83
Sparse Core Ops, SparseCore 0:
  12.8 106.2 all-reduce.2
  129.3 55.2 all-gather.4
  230.7 122.2 all-reduce.4
where the time goes:
time: 362 us; the launch traced here: 361 us
  waiting for transfers between devices  229 us (63%)
  blocking collectives  77.6 us (21%)
  local copies, waits for them, and re-layouts  22.3 us (6%)
  between operations  13.2 us (4%)
  matrix products  12.6 us (3%)
  other arithmetic  5.93 us (2%)
    psum x1, waiting for transfers between devices, body(): return lax.psum(partial_out, ('seq', 'head'))  122 us
    psum x1, waiting for transfers between devices, body(): query = lax.psum(partial_query, 'seq')  107 us
    all_gather x2, blocking collectives, joined(): gathered = jax.tree.map(lambda a: lax.all_gather(a, axis), part)  77.6 us
    dynamic_slice x18, local copies, waits for them, and re-layouts, take(): lax.dynamic_index_in_dim(a, source, 0, False)  13.5 us
  transfers between devices with their start and end apart: 3, of which 2 were waited for; matrix products, arithmetic and copies ran while one was open for 1% of the time, Pallas kernels for 0%

commit v1 on v0

--- a/solution.py
+++ b/solution.py
@@ -1,3 +1,4 @@
+import functools
 import math
 import jax
 import jax.numpy as jnp
@@ -10,6 +11,18 @@
 KPG = 4
 REP = 4
 QW = 2048
+
+
+def prepare_cycles(q_in, mesh_name):
+    fan = lax.psum(1, axis_name=mesh_name)
+    last = q_in
+    for i0 in [[(s, s ^ h) for s in range(fan)] for h in (1, 2, 4, 8, 16) if h < fan]:
+        front = lax.ppermute(last, mesh_name, perm=i0)
+        last = last + front
+    return last
+
+
+wrap_record_here = functools.partial(prepare_cycles, mesh_name="seq")
 
 
 def joined(part, axis, combine):
@@ -51,7 +64,7 @@
     dim_rows = query_weight.shape[0]
     state_rows = lax.dynamic_slice_in_dim(hidden_state, seq_index * dim_rows, dim_rows, 1)
     partial_query = jnp.dot(state_rows, query_weight[:, 0, :], preferred_element_type=jnp.float32)
-    query = lax.psum(partial_query, "seq")
+    query = wrap_record_here(partial_query)
     query_heads = query.reshape(batch, KPG, REP, HD)
     keys_lat = latent_key[:, :, 0, :]
     values_lat = latent_value[:, :, 0, :]

time: 362 us -> 273 us (0.75)
  waiting for transfers between devices: 229 us -> 128 us
  starting transfers between devices: 0.09 us -> 10.7 us
    psum x1 -> x0, waiting for transfers between devices: 107 us -> none  [body(): query = lax.psum(partial_query, 'seq')]
    ppermute x0 -> x4, starting transfers between devices: none -> 10.7 us  [prepare_cycles(): front = lax.ppermute(last, mesh_name, perm=i0)]
    ppermute x0 -> x4, waiting for transfers between devices: none -> 6.05 us  [prepare_cycles(): front = lax.ppermute(last, mesh_name, perm=i0)]
  transfers between devices with their start and end apart: 3 -> 6, of which waited for: 2 -> 4; matrix products, arithmetic and copies ran while one was open for 1% -> 2% of each run, Pallas kernels for 0% -> 0%
where the time goes in v1:
time: 273 us; the launch traced here: 272 us
  waiting for transfers between devices  128 us (47%)
  blocking collectives  79.8 us (29%)
  local copies, waits for them, and re-layouts  21.6 us (8%)
  between operations  13.5 us (5%)
  matrix products  11.8 us (4%)
  starting transfers between devices  10.7 us (4%)
  other arithmetic  5.96 us (2%)
    psum x1, waiting for transfers between devices, body(): return lax.psum(partial_out, ('seq', 'head'))  122 us
    all_gather x2, blocking collectives, joined(): gathered = jax.tree.map(lambda a: lax.all_gather(a, axis), part)  79.8 us
    dynamic_slice x18, local copies, waits for them, and re-layouts, take(): lax.dynamic_index_in_dim(a, source, 0, False)  13.5 us
    ppermute x4, starting transfers between devices, prepare_cycles(): front = lax.ppermute(last, mesh_name, perm=i0)  10.7 us
    ppermute x4, waiting for transfers between devices, prepare_cycles(): front = lax.ppermute(last, mesh_name, perm=i0)  6.05 us
    dot_general x1, matrix products, body(): jnp.einsum('bjre,bce->bjrc', query_latent, keys_lat.astype(jnp.float32),...  5.88 us
  transfers between devices with their start and end apart: 6, of which 4 were waited for; matrix products, arithmetic and copies ran while one was open for 2% of the time, Pallas kernels for 0%

profile of v1, /device:TPU:0, one launch (start us, length us, event | category | flops | bytes accessed | tf_op | source)
XLA Modules:
  0.0 271.7 jit_solution(16732586622730276703)
XLA Ops:
  6.5 1.6 fusion.13
  8.1 3.0 %collective-permute-start = (f32[8,2048]{1,0:T(8,128)S(1)}, f32[8,2048]{1,0:T(8,128)S(1)}, u32[]{:S(2)}, u32[]{:S(2)}) collective-permute-start(f32[8,2048]{1,0:T(8,128)S(1)} %fusion.13), channel_id=1, source_target_pairs={{0,2},{2,0},{4,6},{6,4},{8,10},{10,8},{12,14},{14,12},{16,18},{18,... | collective-permute-start | bytes 196616 | tf_op jit(solution)/shard_map/ppermute | solution.py:20
  11.1 2.2 collective-permute-done
  13.3 2.1 collective-permute-start.1
  15.5 0.7 broadcast_compare_fusion
  16.1 1.6 collective-permute-done.1
  17.7 2.1 collective-permute-start.2
  19.9 2.2 collective-permute-done.2
  22.1 3.4 %collective-permute-start.3 = (f32[8,2048]{1,0:T(8,128)S(1)}, f32[8,2048]{1,0:T(8,128)S(1)}, u32[]{:S(2)}, u32[]{:S(2)}) collective-permute-start(f32[8,2048]{1,0:T(8,128)S(1)} %add.95), channel_id=1, source_target_pairs={{0,16},{2,18},{4,20},{6,22},{8,24},{10,26},{12,28},{14,30},{16,0},... | collective-permute-start | bytes 196616 | tf_op jit(solution)/shard_map/ppermute | solution.py:20
  25.6 0.7 compare_and_fusion
  26.4 1.0 reshape.54
  27.4 1.0 reshape.55
  28.5 0.4 convolution_bitcast_fusion
  28.8 5.9 %select_reduce_fusion = (f32[8,4,4]{2,1,0:T(4,128)S(1)}, f32[8,4,4,1024]{3,2,1,0:T(4,128)S(1)}) fusion(pred[8,1024]{1,0:T(8,128)(4,1)S(1)} %compare_and_fusion, f32[8,4,4,256]{3,2,1,0:T(4,128)S(1)} %convolution_bitcast_fusion, bf16[8,1024,1,256]{3,1,2,0:T(8,128)(2,1)} %param.15), kind=kOutput, calls=%fused_computation.22 | convolution fusion | flops 403046272 | bytes 4858368 | tf_op jit(solution)/shard_map/bjre,bce->bjrc/dot_general | solution.py:80
  34.7 2.1 fusion.4
  36.8 0.9 convolution_bitcast_fusion.1
  37.8 42.4 %all-gather = f32[128,4,4]{2,1,0:T(4,128)S(1)} all-gather(f32[8,4,4]{2,1,0:T(4,128)S(1)} %get-tuple-element.223), channel_id=2, replica_groups=mesh['seq'=16,'head'=2] {'seq'}, dimensions={0}, use_global_device_ids=true | all-gather | bytes 8704 | tf_op jit(solution)/shard_map/all_gather | solution.py:29
  80.3 0.5 copy.37
  80.8 0.4 fusion.15
  81.2 37.4 %all-gather.1 = f32[128,4,4]{2,1,0:T(4,128)S(1)} all-gather(f32[8,4,4]{2,1,0:T(4,128)S(1)} %fusion.15), channel_id=3, replica_groups=mesh['seq'=16,'head'=2] {'seq'}, dimensions={0}, use_global_device_ids=true | all-gather | bytes 8704 | tf_op jit(solution)/shard_map/all_gather | solution.py:29
  118.7 0.5 copy.38
  119.2 0.8 slice.8
  120.0 20.1 %while.19 = (s32[]{:T(128)}, f32[8,4,4]{0,2,1:T(4,128)S(1)}, f32[8,4,4]{0,2,1:T(4,128)S(1)}, f32[8,4,4,128]{3,2,1,0:T(4,128)S(1)}, f32[16,8,4,4]{1,3,2,0:T(4,128...) while((s32[]{:T(128)}, f32[8,4,4]{0,2,1:T(4,128)S(1)}, ...), condition=%wide.region_3.4_spmd, body=%wide.region_2.3_spmd.sunk | while | flops 49925 | bytes 334991 | solution.py:34
  120.3 0.8 constant_dynamic-slice_fusion.2
  121.1 0.2 fusion.34
  121.6 0.8 constant_dynamic-slice_fusion.2
  122.5 0.2 fusion.34
  123.0 0.8 constant_dynamic-slice_fusion.2
  123.8 0.2 fusion.34
  124.3 0.8 constant_dynamic-slice_fusion.2
  125.2 0.2 fusion.34
  125.7 0.8 constant_dynamic-slice_fusion.2
  127.0 0.8 constant_dynamic-slice_fusion.2
  128.3 0.8 constant_dynamic-slice_fusion.2
  129.7 0.8 constant_dynamic-slice_fusion.2
  131.0 0.8 constant_dynamic-slice_fusion.2
  131.9 0.2 fusion.34
  132.3 0.8 constant_dynamic-slice_fusion.2
  133.7 0.8 constant_dynamic-slice_fusion.2
  135.0 0.8 constant_dynamic-slice_fusion.2
  135.9 0.2 fusion.34
  136.4 0.8 constant_dynamic-slice_fusion.2
  137.7 0.8 constant_dynamic-slice_fusion.2
  139.0 0.8 constant_dynamic-slice_fusion.2
  139.9 0.2 fusion.34
  140.4 0.9 fusion.11
  141.3 122.0 %all-reduce.2.cloned.1.call-done = f32[8,4096]{1,0:T(8,128)} async-done(((f32[8,4096]{1,0:T(8,128)}), f32[8,4096]{1,0:T(8,128)}) %all-reduce.2.cloned.1.call-update) | async-done | bytes 131088 | tf_op jit(solution)/shard_map/psum | solution.py:96
  263.3 1.6 copy.85
  (77 shorter events, 6.2 us)
Async XLA Ops:
  6.5 133.9 %copy-start = (bf16[1,128,4096]{2,1,0:T(8,128)(2,1)S(1)}, bf16[1,128,4096]{2,1,0:T(8,128)(2,1)}, u32[]{:S(2)}) copy-start(bf16[1,128,4096]{2,1,0:T(8,128)(2,1)} %param.19) | copy-start | bytes 3145732
  6.5 112.6 %all-gather.5.cloned.1.call-start = ((), (), s32[]{:S(2)}) async-start(), calls=%async_computation.1 | async-start | bytes 1114112 | tf_op jit(solution)/shard_map/all_gather | solution.py:29
  8.1 5.2 %collective-permute-start = (f32[8,2048]{1,0:T(8,128)S(1)}, f32[8,2048]{1,0:T(8,128)S(1)}, u32[]{:S(2)}, u32[]{:S(2)}) collective-permute-start(f32[8,2048]{1,0:T(8,128)S(1)} %fusion.13), channel_id=1, source_target_pairs={{0,2},{2,0},{4,6},{6,4},{8,10},{10,8},{12,14},{14,12},{16,18},{18,... | collective-permute-start | bytes 196616 | tf_op jit(solution)/shard_map/ppermute | solution.py:20
  13.3 4.4 %collective-permute-start.1 = (f32[8,2048]{1,0:T(8,128)S(1)}, f32[8,2048]{1,0:T(8,128)S(1)}, u32[]{:S(2)}, u32[]{:S(2)}) collective-permute-start(f32[8,2048]{1,0:T(8,128)S(1)} %add.93), channel_id=1, source_target_pairs={{0,4},{2,6},{4,0},{6,2},{8,12},{10,14},{12,8},{14,10},{16,20},{18,... | collective-permute-start | bytes 196616 | tf_op jit(solution)/shard_map/ppermute | solution.py:20
  17.7 4.4 %collective-permute-start.2 = (f32[8,2048]{1,0:T(8,128)S(1)}, f32[8,2048]{1,0:T(8,128)S(1)}, u32[]{:S(2)}, u32[]{:S(2)}) collective-permute-start(f32[8,2048]{1,0:T(8,128)S(1)} %add.94), channel_id=1, source_target_pairs={{0,8},{2,10},{4,12},{6,14},{8,0},{10,2},{12,4},{14,6},{16,24},{18,... | collective-permute-start | bytes 196616 | tf_op jit(solution)/shard_map/ppermute | solution.py:20
  22.1 6.3 %collective-permute-start.3 = (f32[8,2048]{1,0:T(8,128)S(1)}, f32[8,2048]{1,0:T(8,128)S(1)}, u32[]{:S(2)}, u32[]{:S(2)}) collective-permute-start(f32[8,2048]{1,0:T(8,128)S(1)} %add.95), channel_id=1, source_target_pairs={{0,16},{2,18},{4,20},{6,22},{8,24},{10,26},{12,28},{14,30},{16,0},... | collective-permute-start | bytes 196616 | tf_op jit(solution)/shard_map/ppermute | solution.py:20
  28.4 6.3 %copy-start.1 = (bf16[8,1024,1,256]{3,1,2,0:T(8,128)(2,1)S(1)}, bf16[8,1024,1,256]{3,1,2,0:T(8,128)(2,1)}, u32[]{:S(2)}) copy-start(bf16[8,1024,1,256]{3,1,2,0:T(8,128)(2,1)} %param.16) | copy-start | bytes 12582916
  37.8 225.5 %all-reduce.2.cloned.1.call-start = ((), (), s32[]{:S(2)}) async-start(), calls=%async_computation | async-start | bytes 262144 | tf_op jit(solution)/shard_map/psum | solution.py:96
Sparse Core Ops, SparseCore 0:
  37.9 56.6 all-gather.4
  141.5 121.7 all-reduce.1
